TPU v7x, 32 devices: a whole 2x2x4 slice. The times are simulated.
32 devices in a mesh: front: 2 (over core), row: 4 (over y, x), col: 4 (over z).
Axes of the slice: x: 2, y: 2, z: 4, core: 2. Of those that a mesh axis runs over, the one named last changes fastest.
Arguments:
- front_rows: float32 [4096, 24576], P(('front', 'row'), 'col'), parts along dimension 0, may hold values from -0.0546875 to 0.0546875
- random_columns: bfloat16 [49152, 512], P(('front', 'col'), 'row'), parts along dimension 0, may hold values from -6 to 6
Outputs:
- basis: float32 [4096, 256], P(('front', 'row', 'col')), parts along dimension 0
- projected: float32 [1024, 512], P(('front', 'row')), parts along dimension 0
There are 2 independent parts, one for each index of `front`. A program takes and returns all parts, laid end to end along the dimension named above; each array names one. Nothing has to cross between parts.
All inputs are finite; a program needn't handle non-finite values.
Results may differ from a plain program's by a relative error of at most 0.0003.
Values may be sent and summed in bfloat16 or wider, within the bound.
A program may use at most 64 MiB of HBM per device.

v0:
```python
import jax
import jax.numpy as jnp
from jax import lax
from jax.sharding import PartitionSpec as P

RANK = 256


def partner(value, axis, stride):
    mask = 2**stride
    pairs = [(source, source ^ mask) for source in range(lax.axis_size(axis))]
    return lax.ppermute(value, axis, pairs)


def inner_rows(left, right):
    return lax.dot_general(
        left,
        right,
        (((0,), (0,)), ((), ())),
        precision=lax.Precision.HIGHEST,
        preferred_element_type=jnp.float32,
    )


def leaf_total(partial_gram):
    return partial_gram + partner(partial_gram, "row", 0)


def per_device(front_rows, random_columns):
    block_rows = front_rows.shape[0]
    col_count = lax.axis_size("col")
    col_index = lax.axis_index("col")
    row_index = lax.axis_index("row")
    own_rows = block_rows // col_count
    partial_value = jnp.dot(
        front_rows,
        lax.all_gather(random_columns, "row", axis=1, tiled=True).astype(jnp.float32),
        precision=lax.Precision.HIGHEST,
        preferred_element_type=jnp.float32,
    )
    whole = lax.psum(partial_value, "col")
    local_gram = inner_rows(whole[:, :RANK], whole)
    mine = lax.dynamic_slice_in_dim(whole, col_index * own_rows, own_rows, 0)
    gram = leaf_total(local_gram)
    lower = jnp.linalg.cholesky(gram[:, :RANK])
    basis = lax.linalg.triangular_solve(
        lower, mine[:, :RANK], left_side=False, lower=True, transpose_a=True
    )
    coupling = lax.linalg.triangular_solve(lower, gram, left_side=True, lower=True)
    half = RANK // 2
    projected = lax.dynamic_slice_in_dim(coupling, row_index % 2 * half, half, 0)
    return (basis, projected)


def solution(mesh):
    return jax.shard_map(
        per_device,
        mesh=mesh,
        in_specs=(P(("front", "row"), "col"), P(("front", "col"), "row")),
        out_specs=(P(("front", "row", "col"), None), P(("front", "row"), None)),
        check_vma=False,
    )
```

profile of v0, /device:TPU:0, one launch (start us, length us, event | category | flops | bytes accessed | tf_op | source)
XLA Modules:
  0.0 239.0 jit_solution(649683142217514492)
XLA Ops:
  7.2 0.7 all-gather.2.cloned.1.call-update
  7.9 74.5 %all-gather.2.cloned.1.call-done = bf16[6144,512]{1,0:T(8,128)(2,1)} async-done(((bf16[6144,128]{1,0:T(8,128)(2,1)}), bf16[6144,512]{1,0:T(8,128)(2,1)}) %all-gather.2.cloned.1.call-update) | async-done | bytes 6291472 | tf_op jit(solution)/shard_map/all_gather | solution.py:37
  82.4 14.8 %fusion.18 = f32[512,512]{1,0:T(8,128)} fusion(f32[512,6144]{1,0:T(8,128)} %param.2, bf16[6144,512]{1,0:T(8,128)(2,1)} %all-gather.2.cloned.1.call-done), kind=kOutput, calls=%fused_computation.41 | convolution fusion | flops 19327352832 | bytes 19922944 | tf_op jit(solution)/shard_map/dot_general | solution.py:35
  97.3 52.1 %all-reduce.3.cloned.1.call-done = f32[512,512]{1,0:T(8,128)} async-done(((f32[512,512]{1,0:T(8,128)}), f32[512,512]{1,0:T(8,128)}) %all-reduce.3.cloned.1.call-update) | async-done | bytes 1048592 | tf_op jit(solution)/shard_map/psum | solution.py:41
  149.3 3.2 %fusion = f32[256,512]{0,1:T(8,128)S(1)} fusion(f32[512,512]{1,0:T(8,128)} %all-reduce.3.cloned.1.call-done), kind=kOutput, calls=%fused_computation.4 | convolution fusion | flops 805306368 | bytes 2097152 | tf_op jit(solution)/shard_map/dot_general | solution.py:16
  152.5 1.5 collective-permute-start
  154.1 12.3 %collective-permute-done = f32[256,512]{0,1:T(8,128)S(1)} collective-permute-done((f32[256,512]{0,1:T(8,128)S(1)}, f32[256,512]{0,1:T(8,128)S(1)}, u32[]{:S(2)}, u32[]{:S(2)}) %collective-permute-start) | collective-permute-done | bytes 524320 | tf_op jit(solution)/shard_map/ppermute | solution.py:12
  166.7 11.7 %cholesky.50 = f32[128,128]{1,0:T(8,128)S(1)} custom-call(f32[128,128]{1,0:T(8,128)S(1)} %cholesky.118), custom_call_target="Cholesky" | custom-call | tf_op jit(solution)/shard_map/jit(cholesky)/cholesky | solution.py:45
  178.4 9.8 %custom-call.16 = f32[1,128,128]{1,2,0:T(8,128)S(1)} custom-call(f32[1,128,128]{2,1,0:T(8,128)S(1)} %get-tuple-element.25), custom_call_target="InvertDiagBlocksLowerTriangular" | custom-call | tf_op jit(solution)/shard_map/jit(cholesky)/cholesky | solution.py:45
  188.7 11.9 %cholesky.105 = f32[128,128]{1,0:T(8,128)S(1)} custom-call(f32[128,128]{1,0:T(8,128)S(1)} %convolution_subtract_fusion.1), custom_call_target="Cholesky" | custom-call | tf_op jit(solution)/shard_map/jit(cholesky)/cholesky | solution.py:45
  200.6 0.7 compare_reduce_fusion
  202.8 4.1 %while.1 = (s32[]{:T(128)}, f32[256,256]{1,0:T(8,128)S(1)}, s32[2,2]{1,0:T(2,128)S(1)}, f32[2,128,128]{2,1,0:T(8,128)S(1)}, s32[]{:T(128)}) while((s32[]{:T(128)}, f32[256,256]{1,0:T(8,128)S(1)}, s32[2,2]{1,0:T(2,128)S(1)}, f32[2,128,128]{2,1,0:T(8,128)S(1)}, s32[]{:T(128)}) %tuple.28), condition=%wide.while_cond, body=%wide.while_body.sunk | while | flops 2 | bytes 131181 | solution.py:46
  202.8 0.6 fusion.28
  203.4 1.4 bitcast_dynamic-update-slice_fusion.2
  204.9 0.6 fusion.28
  205.5 1.4 bitcast_dynamic-update-slice_fusion.2
  206.9 19.7 %custom-call.17 = f32[2,128,128]{1,2,0:T(8,128)S(1)} custom-call(f32[2,128,128]{2,1,0:T(8,128)S(1)} %get-tuple-element.9), custom_call_target="InvertDiagBlocksLowerTriangular" | custom-call | tf_op jit(solution)/shard_map/triangular_solve | solution.py:46
  226.6 0.4 fusion.4
  227.0 0.6 fusion.13
  227.6 0.4 fusion.3
  228.0 1.1 fusion.9
  229.2 1.1 convolution_subtract_fusion
  230.6 0.8 copy.7
  231.4 0.8 fusion.2
  (21 shorter events, 1.3 us)
Async XLA Ops:
  7.2 75.3 %all-gather.2.cloned.1.call-start = ((), (), s32[]{:S(2)}) async-start(), calls=%async_computation | async-start | bytes 7864320 | tf_op jit(solution)/shard_map/all_gather | solution.py:37
  7.9 141.4 %all-reduce.3.cloned.1.call-start = ((), (), s32[]{:S(2)}) async-start(), calls=%async_computation.1 | async-start | bytes 2097152 | tf_op jit(solution)/shard_map/psum | solution.py:41
  152.5 13.8 %collective-permute-start = (f32[256,512]{0,1:T(8,128)S(1)}, f32[256,512]{0,1:T(8,128)S(1)}, u32[]{:S(2)}, u32[]{:S(2)}) collective-permute-start(f32[256,512]{0,1:T(8,128)S(1)} %fusion), channel_id=1, source_target_pairs={{0,4},{4,0},{8,12},{12,8},{1,5},{5,1},{9,13},{13,9},{2,6},{6,2},{1... | collective-permute-start | bytes 1572872 | tf_op jit(solution)/shard_map/ppermute | solution.py:12
Sparse Core Ops, SparseCore 0:
  9.8 72.6 all-gather.1
  97.4 51.8 all-reduce.2
where the time goes:
time: 239 us
  waiting for transfers between devices  140 us (59%)
  other arithmetic  54.7 us (23%)
  matrix products  22.5 us (9%)
  between operations  15.5 us (6%)
  local copies, waits for them, and re-layouts  5.06 us (2%)
    all_gather x1, waiting for transfers between devices, per_device(): lax.all_gather(random_columns, 'row', axis=1, tiled=True)  74.5 us
    psum x1, waiting for transfers between devices, per_device(): whole = lax.psum(partial_value, 'col')  52.1 us
    another operation x6, other arithmetic, per_device(): lower = jnp.linalg.cholesky(gram[:, :RANK])  34.2 us
    another operation x4, other arithmetic, per_device(): lax.linalg.triangular_solve(lower, mine[:, :RANK], left_side=False, lower...  19.7 us
    dot_general x1, matrix products, per_device(): jnp.dot(front_rows, lax.all_gather(random_columns, 'row', axis=1, tiled=T...  14.8 us
    ppermute x1, waiting for transfers between devices, partner(): return lax.ppermute(value, axis, pairs)  12.3 us
  transfers between devices with their start and end apart: 3, of which 3 were waited for; matrix products, arithmetic and copies ran while one was open for 0% of the time, Pallas kernels for 0%

commit v1 on v0

--- a/solution.py
+++ b/solution.py
@@ -38,7 +38,7 @@
         precision=lax.Precision.HIGHEST,
         preferred_element_type=jnp.float32,
     )
-    whole = lax.psum(partial_value, "col")
+    whole = jnp.sum(lax.all_gather(partial_value, "col"), axis=0)
     local_gram = inner_rows(whole[:, :RANK], whole)
     mine = lax.dynamic_slice_in_dim(whole, col_index * own_rows, own_rows, 0)
     gram = leaf_total(local_gram)

time: 239 us -> 268 us (1.12)
  waiting for transfers between devices: 140 us -> 168 us
  matrix products: 22.5 us -> 19.4 us
  other arithmetic: 54.7 us -> 57.6 us
    all_gather x0 -> x1, waiting for transfers between devices: none -> 80.9 us  [per_device(): whole = jnp.sum(lax.all_gather(partial_value, 'col'), axis=0)]
    psum x1 -> x0, waiting for transfers between devices: 52.1 us -> none  [per_device(): whole = lax.psum(partial_value, 'col')]
    reduce_sum x0 -> x1, other arithmetic: none -> 2.78 us  [per_device(): whole = jnp.sum(lax.all_gather(partial_value, 'col'), axis=0)]
where the time goes in v1:
time: 268 us; the launch traced here: 267 us
  waiting for transfers between devices  168 us (63%)
  other arithmetic  57.6 us (21%)
  matrix products  19.4 us (7%)
  between operations  15.5 us (6%)
  local copies, waits for them, and re-layouts  5.06 us (2%)
    all_gather x1, waiting for transfers between devices, per_device(): whole = jnp.sum(lax.all_gather(partial_value, 'col'), axis=0)  80.9 us
    all_gather x1, waiting for transfers between devices, per_device(): lax.all_gather(random_columns, 'row', axis=1, tiled=True)  74.5 us
    another operation x6, other arithmetic, per_device(): lower = jnp.linalg.cholesky(gram[:, :RANK])  34.2 us
    another operation x4, other arithmetic, per_device(): lax.linalg.triangular_solve(lower, mine[:, :RANK], left_side=False, lower...  19.7 us
    dot_general x1, matrix products, per_device(): jnp.dot(front_rows, lax.all_gather(random_columns, 'row', axis=1, tiled=T...  14.8 us
    ppermute x1, waiting for transfers between devices, partner(): return lax.ppermute(value, axis, pairs)  12.1 us
  transfers between devices with their start and end apart: 3, of which 3 were waited for; matrix products, arithmetic and copies ran while one was open for 0% of the time, Pallas kernels for 0%

profile of v1, /device:TPU:0, one launch (start us, length us, event | category | flops | bytes accessed | tf_op | source)
XLA Modules:
  0.0 267.4 jit_solution(3443054238204044259)
XLA Ops:
  7.2 0.7 all-gather.4.cloned.1.call-update
  7.9 74.5 %all-gather.4.cloned.1.call-done = bf16[6144,512]{1,0:T(8,128)(2,1)} async-done(((bf16[6144,128]{1,0:T(8,128)(2,1)}), bf16[6144,512]{1,0:T(8,128)(2,1)}) %all-gather.4.cloned.1.call-update) | async-done | bytes 6291472 | tf_op jit(solution)/shard_map/all_gather | solution.py:37
  82.4 14.8 %fusion.18 = f32[512,512]{1,0:T(8,128)} fusion(f32[512,6144]{1,0:T(8,128)} %param.2, bf16[6144,512]{1,0:T(8,128)(2,1)} %all-gather.4.cloned.1.call-done), kind=kOutput, calls=%fused_computation.41 | convolution fusion | flops 19327352832 | bytes 19922944 | tf_op jit(solution)/shard_map/dot_general | solution.py:35
  97.3 80.9 %all-gather.6.cloned.1.call-done = f32[2048,512]{1,0:T(8,128)} async-done(((f32[512,512]{1,0:T(8,128)}), f32[2048,512]{1,0:T(8,128)}) %all-gather.6.cloned.1.call-update) | async-done | bytes 4194320 | tf_op jit(solution)/shard_map/all_gather | solution.py:41
  178.2 2.8 %reduce_sum.9 = f32[512,512]{1,0:T(8,128)S(1)} reduce(f32[4,512,512]{2,1,0:T(8,128)} %bitcast.38, f32[]{:T(128)} %constant.97.clone.1), dimensions={0}, to_apply=%region_0.0 | reduce | flops 786432 | bytes 5242884 | tf_op jit(solution)/shard_map/reduce_sum | solution.py:41
  180.9 1.8 fusion
  182.8 1.5 collective-permute-start
  184.3 12.1 %collective-permute-done = f32[256,512]{0,1:T(8,128)S(1)} collective-permute-done((f32[256,512]{0,1:T(8,128)S(1)}, f32[256,512]{0,1:T(8,128)S(1)}, u32[]{:S(2)}, u32[]{:S(2)}) %collective-permute-start) | collective-permute-done | bytes 524320 | tf_op jit(solution)/shard_map/ppermute | solution.py:12
  196.7 11.7 %cholesky.50 = f32[128,128]{1,0:T(8,128)S(1)} custom-call(f32[128,128]{1,0:T(8,128)S(1)} %cholesky.118), custom_call_target="Cholesky" | custom-call | tf_op jit(solution)/shard_map/jit(cholesky)/cholesky | solution.py:45
  208.4 9.8 %custom-call.16 = f32[1,128,128]{1,2,0:T(8,128)S(1)} custom-call(f32[1,128,128]{2,1,0:T(8,128)S(1)} %get-tuple-element.25), custom_call_target="InvertDiagBlocksLowerTriangular" | custom-call | tf_op jit(solution)/shard_map/jit(cholesky)/cholesky | solution.py:45
  218.7 11.9 %cholesky.105 = f32[128,128]{1,0:T(8,128)S(1)} custom-call(f32[128,128]{1,0:T(8,128)S(1)} %convolution_subtract_fusion.1), custom_call_target="Cholesky" | custom-call | tf_op jit(solution)/shard_map/jit(cholesky)/cholesky | solution.py:45
  230.7 0.7 compare_reduce_fusion
  232.9 4.1 %while.1 = (s32[]{:T(128)}, f32[256,256]{1,0:T(8,128)S(1)}, s32[2,2]{1,0:T(2,128)S(1)}, f32[2,128,128]{2,1,0:T(8,128)S(1)}, s32[]{:T(128)}) while((s32[]{:T(128)}, f32[256,256]{1,0:T(8,128)S(1)}, s32[2,2]{1,0:T(2,128)S(1)}, f32[2,128,128]{2,1,0:T(8,128)S(1)}, s32[]{:T(128)}) %tuple.28), condition=%wide.while_cond, body=%wide.while_body.sunk | while | flops 2 | bytes 131181 | solution.py:46
  232.9 0.6 fusion.28
  233.5 1.4 bitcast_dynamic-update-slice_fusion.2
  234.9 0.6 fusion.28
  235.5 1.4 bitcast_dynamic-update-slice_fusion.2
  237.0 19.7 %custom-call.17 = f32[2,128,128]{1,2,0:T(8,128)S(1)} custom-call(f32[2,128,128]{2,1,0:T(8,128)S(1)} %get-tuple-element.9), custom_call_target="InvertDiagBlocksLowerTriangular" | custom-call | tf_op jit(solution)/shard_map/triangular_solve | solution.py:46
  256.6 0.4 fusion.4
  257.1 0.6 fusion.13
  257.7 0.4 fusion.3
  258.4 0.3 convolution_subtract_fusion
  259.0 0.8 copy.7
  259.8 0.8 fusion.2
  (22 shorter events, 1.6 us)
Async XLA Ops:
  7.2 75.3 %all-gather.4.cloned.1.call-start = ((), (), s32[]{:S(2)}) async-start(), calls=%async_computation | async-start | bytes 7864320 | tf_op jit(solution)/shard_map/all_gather | solution.py:37
  7.9 170.3 %all-gather.6.cloned.1.call-start = ((), (), s32[]{:S(2)}) async-start(), calls=%async_computation.1 | async-start | bytes 5242880 | tf_op jit(solution)/shard_map/all_gather | solution.py:41
  182.8 13.6 %collective-permute-start = (f32[256,512]{0,1:T(8,128)S(1)}, f32[256,512]{0,1:T(8,128)S(1)}, u32[]{:S(2)}, u32[]{:S(2)}) collective-permute-start(f32[256,512]{0,1:T(8,128)S(1)} %fusion), channel_id=1, source_target_pairs={{0,4},{4,0},{8,12},{12,8},{1,5},{5,1},{9,13},{13,9},{2,6},{6,2},{1... | collective-permute-start | bytes 1572872 | tf_op jit(solution)/shard_map/ppermute | solution.py:12
Sparse Core Ops, SparseCore 0:
  9.8 72.6 all-gather.3
  97.4 80.7 all-gather.5
